TPU v7x, 32 devices: a whole 2x2x4 slice. The times are simulated.
32 devices in a mesh: blk: 16 (over z, y, x), edge: 2 (over core).
Axes of the slice: x: 2, y: 2, z: 4, core: 2. Of those that a mesh axis runs over, the one named last changes fastest.
Arguments:
- node_feat: bfloat16 [512, 128], P(('blk', 'edge')), may hold values from -6 to 6
- coords: bfloat16 [3, 512], P(None, ('blk', 'edge')), may hold values from -4 to 4
- pair_table: int32 [3, 16], replicated, may hold values from 0 to 15, as said below
- w_tgt: bfloat16 [128, 128], replicated, may hold values from -0.375 to 0.375
- w_src: bfloat16 [128, 128], replicated, may hold values from -0.375 to 0.375
- w_dist: float32 [128], replicated, may hold values from -0.8 to 0.8
- edge_bias: float32 [128], replicated, may hold values from -2 to 2
- w_edge: bfloat16 [128, 128], replicated, may hold values from -0.5 to 0.5
- w_gate: float32 [128], replicated, may hold values from -1.5 to 1.5
- w_coord: bfloat16 [128, 128], replicated, may hold values from -0.5 to 0.5
- w_weight: float32 [128], replicated, may hold values from -5 to 5
- w_node_in: bfloat16 [256, 128], replicated, may hold values from -0.375 to 0.375
- w_node_out: bfloat16 [128, 128], replicated, may hold values from -0.5 to 0.5
Outputs:
- new_feat: bfloat16 [512, 128], P(('blk', 'edge'))
- new_coords: float32 [3, 512], P(None, ('blk', 'edge'))
Inputs may be any that keep to these rules, and one draw needn't show every extreme that they name: Each row pairs the 16 blocks: pair_table[r, b] = c exactly when pair_table[r, c] = b, and c is never b; no block meets the same partner in two rows.
All inputs are finite; a program needn't handle non-finite values.
Results may differ from a plain program's by a relative error of at most 0.0027.
Values may be sent and summed in bfloat16 or wider, within the bound.
No kernel may reach another device: no remote copies, remote signals or barrier semaphores. Data moves between devices by JAX's collectives and lax.ppermute only.
A program may use at most 128 MiB of HBM per device.

v0:
```python
import jax
import jax.numpy as jnp
from jax import lax
from jax.sharding import PartitionSpec as P


def edge_terms(
    tgt_proj,
    tgt_place,
    src_feat,
    src_place,
    keep_mask,
    w_src,
    w_dist,
    edge_bias,
    w_edge,
    w_gate,
    w_coord,
    w_weight,
):
    src_proj = jnp.dot(src_feat, w_src, preferred_element_type=jnp.float32)
    offset = tgt_place.astype(jnp.float32)[:, :, None] - src_place.astype(jnp.float32)[:, None, :]
    radial = jnp.sum(offset * offset, axis=0)
    targets = radial.shape[0]
    sources = radial.shape[1]
    pre_act = tgt_proj[:, None, :] + src_proj[None, :, :] + radial[:, :, None] * w_dist + edge_bias
    hidden = jax.nn.silu(pre_act).astype(jnp.bfloat16).reshape(targets * sources, -1)
    message = jax.nn.silu(jnp.dot(hidden, w_edge, preferred_element_type=jnp.float32))
    edge_gate = (
        jax.nn.sigmoid(jnp.sum(message * w_gate, axis=1)).reshape(targets, sources) * keep_mask
    )
    lifted = jax.nn.silu(
        jnp.dot(message.astype(jnp.bfloat16), w_coord, preferred_element_type=jnp.float32)
    )
    weight = jnp.sum(lifted * w_weight, axis=1).reshape(targets, sources) * keep_mask
    message_sum = jnp.sum(message.reshape(targets, sources, -1) * edge_gate[:, :, None], axis=1)
    unit_dir = offset / (jnp.sqrt(radial) + 1.0)
    coord_sum = jnp.sum(unit_dir * weight[None], axis=2)
    return (message_sum, coord_sum)


def shards(
    node_feat,
    coords,
    pair_table,
    w_tgt,
    w_src,
    w_dist,
    edge_bias,
    w_edge,
    w_gate,
    w_coord,
    w_weight,
    w_node_in,
    w_node_out,
):
    row_count = node_feat.shape[0]
    feat_width = node_feat.shape[1]
    edge_parts = lax.axis_size("edge")
    block_index = lax.axis_index("blk")
    edge_index = lax.axis_index("edge")
    rounds = pair_table.shape[0]
    block_size = row_count * edge_parts
    mean_scale = 1.0 / ((rounds + 1) * block_size - 1)
    weights = (w_src, w_dist, edge_bias, w_edge, w_gate, w_coord, w_weight)
    block_feat, block_place = (
        lax.all_gather(node_feat, "edge", axis=0, tiled=True),
        lax.all_gather(coords, "edge", axis=1, tiled=True),
    )
    partners = lax.dynamic_index_in_dim(pair_table, block_index, 1, keepdims=False)
    tgt_proj = jnp.dot(block_feat, w_tgt, preferred_element_type=jnp.float32)
    target_ids = jnp.arange(block_size, dtype=jnp.int32)
    source_ids = edge_index * row_count + jnp.arange(row_count, dtype=jnp.int32)
    self_keep = (target_ids[:, None] != source_ids[None, :]).astype(jnp.float32)
    all_keep = jnp.ones((block_size, row_count), jnp.float32)
    term_list = [edge_terms(tgt_proj, block_place, node_feat, coords, self_keep, *weights)]
    far_feat, far_place = (
        lax.all_gather(node_feat[None], "blk", axis=0, tiled=True),
        lax.all_gather(coords[None], "blk", axis=0, tiled=True),
    )
    for round_step in range(rounds):
        partner = partners[round_step]
        src_feat = lax.dynamic_index_in_dim(far_feat, partner, 0, keepdims=False)
        src_place = lax.dynamic_index_in_dim(far_place, partner, 0, keepdims=False)
        term_list.append(edge_terms(tgt_proj, block_place, src_feat, src_place, all_keep, *weights))
    message_total = jnp.zeros((row_count, feat_width), jnp.float32)
    coord_total = jnp.zeros((3, row_count), jnp.float32)
    for message_sum, coord_sum in term_list:
        message_part, coord_part = (
            lax.psum_scatter(message_sum, "edge", scatter_dimension=0, tiled=True),
            lax.psum_scatter(coord_sum, "edge", scatter_dimension=1, tiled=True),
        )
        message_total = message_total + message_part
        coord_total = coord_total + coord_part
    message_mean = (message_total * mean_scale).astype(jnp.bfloat16)
    node_pre = jnp.dot(
        node_feat, w_node_in[:feat_width], preferred_element_type=jnp.float32
    ) + jnp.dot(message_mean, w_node_in[feat_width:], preferred_element_type=jnp.float32)
    node_hidden = jax.nn.silu(node_pre).astype(jnp.bfloat16)
    new_feat = (
        node_feat.astype(jnp.float32)
        + jnp.dot(node_hidden, w_node_out, preferred_element_type=jnp.float32)
    ).astype(jnp.bfloat16)
    new_coords = coords.astype(jnp.float32) + coord_total * mean_scale
    return (new_feat, new_coords)


def solution(mesh):
    placed = (
        P(("blk", "edge"), None),
        P(None, ("blk", "edge")),
        P(),
        P(),
        P(),
        P(),
        P(),
        P(),
        P(),
        P(),
        P(),
        P(),
        P(),
    )
    return jax.shard_map(
        shards,
        mesh=mesh,
        in_specs=placed,
        out_specs=(P(("blk", "edge"), None), P(None, ("blk", "edge"))),
        check_vma=False,
    )
```

profile of v0, /device:TPU:0, one launch (start us, length us, event | category | flops | bytes accessed | tf_op | source)
XLA Modules:
  0.0 130.2 jit_solution(1059201408671765147)
XLA Ops:
  7.2 0.7 copy-done.8
  8.0 0.6 fusion.66
  12.6 42.7 %all-gather = bf16[256,128]{1,0:T(8,128)(2,1)S(1)} all-gather(bf16[16,128]{1,0:T(8,128)(2,1)S(1)} %copy-done.2), channel_id=2, replica_groups=mesh['blk'=16,'edge'=2] {'blk'}, dimensions={0}, use_global_device_ids=true | all-gather | bytes 69632 | tf_op jit(solution)/shard_map/all_gather | solution.py:78
  55.4 1.8 %all_gather.12 = bf16[32,128]{1,0:T(8,128)(2,1)S(1)} all-gather(bf16[16,128]{1,0:T(8,128)(2,1)S(1)} %copy-done.2), channel_id=1, replica_groups=mesh['blk'=16,'edge'=2] {'edge'}, dimensions={0}, use_global_device_ids=true | all-gather | bytes 12288 | tf_op jit(solution)/shard_map/all_gather | solution.py:67
  57.2 0.1 fusion.68
  57.9 0.1 fusion.44
  58.8 0.1 fusion.46
  59.6 0.1 fusion.42
  59.7 0.5 copy-done.4
  60.3 35.5 %all-gather.3 = bf16[16,3,16]{2,1,0:T(4,128)(2,1)S(1)} all-gather(bf16[1,3,16]{2,1,0:T(4,128)(2,1)S(1)} %bitcast.97), channel_id=3, replica_groups=mesh['blk'=16,'edge'=2] {'blk'}, dimensions={0}, use_global_device_ids=true | all-gather | bytes 1632 | tf_op jit(solution)/shard_map/all_gather | solution.py:79
  95.8 1.8 %all-gather.2 = bf16[2,16,3]{1,2,0:T(4,128)(2,1)S(1)} all-gather(bf16[1,16,3]{1,2,0:T(4,128)(2,1)S(1)} %bitcast.98), channel_id=1, replica_groups=mesh['blk'=16,'edge'=2] {'edge'}, dimensions={0}, use_global_device_ids=true | all-gather | bytes 288 | tf_op jit(solution)/shard_map/all_gather | solution.py:68
  97.6 0.1 reshape.227
  97.7 0.1 fusion.33
  98.0 0.1 mul.273
  98.1 0.6 copy-done.3
  98.7 0.1 fusion.67
  98.9 0.6 copy-done.6
  99.5 0.2 multiply_convert_fusion.3
  99.8 0.2 fusion.69
  100.0 0.6 copy-done.9
  100.6 0.3 multiply_reduce_fusion.3
  100.9 0.1 reshape.215
  101.1 0.2 fusion.70
  101.2 0.3 multiply_reduce_fusion.2
  101.6 0.1 mul.310
  101.7 0.1 fusion.30
  102.2 0.3 multiply_convert_fusion
  102.4 0.2 fusion.71
  102.6 0.3 multiply_reduce_fusion
  102.9 0.7 copy-done.11
  103.6 0.4 multiply_reduce_fusion.9
  104.0 0.3 multiply_reduce_fusion.1
  104.3 0.1 mul.315
  104.5 0.1 mul.320
  104.6 0.1 fusion.29
  104.8 0.7 copy.63
  105.6 0.2 multiply_reduce_fusion.8
  105.9 0.2 multiply_reduce_fusion.10
  106.1 0.2 multiply_reduce_fusion.6
  106.4 0.2 multiply_reduce_fusion.4
  106.6 0.6 add_add_fusion
  107.2 0.2 copy-done.5
  107.4 0.1 fusion.22
  107.5 3.4 %reduce-scatter.7.cloned.1.call-done = f32[16,3]{1,0:T(8,128)} async-done(((f32[32,3]{1,0:T(8,128)}), f32[16,3]{1,0:T(8,128)}) %reduce-scatter.7.cloned.1.call-update) | async-done | bytes 208
  110.9 0.8 copy.64
  111.7 0.6 multiply_add_fusion
  112.3 9.5 %reduce-scatter.5.cloned.1.call-done = f32[16,128]{1,0:T(8,128)} async-done(((f32[32,128]{1,0:T(8,128)}), f32[16,128]{1,0:T(8,128)}) %reduce-scatter.5.cloned.1.call-update) | async-done | bytes 8208 | tf_op jit(solution)/shard_map/reduce_scatter | solution.py:90
  121.8 1.6 %fusion = bf16[16,128]{1,0:T(8,128)(2,1)} fusion(bf16[128,128]{1,0:T(8,128)(2,1)S(1)} %copy-done.10, f32[16,128]{1,0:T(8,128)S(1)} %fusion.22, bf16[256,128]{1,0:T(8,128)(2,1)S(1)} %copy-done.5, bf16[16,128]{1,0:T(8,128)(2,1)S(1)} %copy-done.2, f32[16,128]{1,0:T(8,128)} %reduce-scatter.5.cloned.1.call-done), kind=kOutput, calls=%fused_computation.2 | convolution fusion | flops 1071104 | bytes 90112 | tf_op jit(solution)/shard_map/dot_general | solution.py:102
  (54 shorter events, 1.6 us)
Async XLA Ops:
  7.2 92.6 %copy-start = (bf16[128,128]{1,0:T(8,128)(2,1)S(1)}, bf16[128,128]{1,0:T(8,128)(2,1)}, u32[]{:S(2)}) copy-start(bf16[128,128]{1,0:T(8,128)(2,1)} %param.20) | copy-start | bytes 98308
  7.2 103.7 %reduce-scatter.7.cloned.1.call-start = ((), (), s32[]{:S(2)}) async-start(), calls=%async_computation.3 | async-start | bytes 24576
  7.2 0.7 copy-start.8
  11.3 1.3 %copy-start.2 = (bf16[16,128]{1,0:T(8,128)(2,1)S(1)}, bf16[16,128]{1,0:T(8,128)(2,1)}, u32[]{:S(2)}) copy-start(bf16[16,128]{1,0:T(8,128)(2,1)} %param.13) | copy-start | bytes 12292
  12.6 44.6 %copy-start.1 = (bf16[128,128]{1,0:T(8,128)(2,1)S(1)}, bf16[128,128]{1,0:T(8,128)(2,1)}, u32[]{:S(2)}) copy-start(bf16[128,128]{1,0:T(8,128)(2,1)} %param.17) | copy-start | bytes 98308
  59.6 0.7 copy-start.4
  97.9 0.8 copy-start.3
  98.9 0.7 copy-start.6
  98.9 0.7 copy-start.7
  99.8 0.8 copy-start.9
  99.8 0.8 copy-start.12
  102.9 0.7 copy-start.11
  105.5 16.3 %reduce-scatter.5.cloned.1.call-start = ((), (), s32[]{:S(2)}) async-start(), calls=%async_computation.2 | async-start | bytes 24576 | tf_op jit(solution)/shard_map/reduce_scatter | solution.py:90
  106.6 0.8 copy-start.5
  107.4 14.4 %copy-start.10 = (bf16[128,128]{1,0:T(8,128)(2,1)S(1)}, bf16[128,128]{1,0:T(8,128)(2,1)}, u32[]{:S(2)}) copy-start(bf16[128,128]{1,0:T(8,128)(2,1)} %param.25) | copy-start | bytes 98308
Sparse Core Ops, SparseCore 0:
  105.6 5.2 reduce-scatter.6
  113.1 8.6 reduce-scatter.4
where the time goes:
time: 131 us; the launch traced here: 130 us
  blocking collectives  81.9 us (63%)
  between operations  20.3 us (15%)
  waiting for transfers between devices  12.9 us (10%)
  local copies, waits for them, and re-layouts  7.69 us (6%)
  matrix products  4.56 us (3%)
  other arithmetic  2.76 us (2%)
    all_gather x1, blocking collectives, shards(): lax.all_gather(node_feat[None], 'blk', axis=0, tiled=True)  42.7 us
    all_gather x1, blocking collectives, shards(): lax.all_gather(coords[None], 'blk', axis=0, tiled=True)  35.5 us
    reduce_scatter x1, waiting for transfers between devices, shards(): lax.psum_scatter(message_sum, 'edge', scatter_dimension=0, tiled=True)  9.48 us
    unnamed x28, local copies, waits for them, and re-layouts  5.39 us
    unnamed x3, waiting for transfers between devices  3.42 us
  transfers between devices with their start and end apart: 2, of which 2 were waited for; matrix products, arithmetic and copies ran while one was open for 2% of the time, Pallas kernels for 0%

commit v1 on v0

v1 whole, which is shorter than its diff:
```python
import jax
import jax.numpy as jnp
from jax import lax
from jax.experimental import pallas as pl
from jax.experimental.pallas import tpu as pltpu
from jax.sharding import PartitionSpec as P

F32 = jnp.float32
BF16 = jnp.bfloat16
LANES = 128


def split2(x):
    hi = x.astype(BF16)
    lo = (x - hi.astype(F32)).astype(BF16)
    return hi, lo


def dot(a, b):
    return jnp.dot(a, b, preferred_element_type=F32)


def half_silu(h):
    return h + h * jnp.tanh(h)


def prep_body(
    feat,
    coords,
    w_tgt,
    w_src,
    w_dist,
    edge_bias,
    w_edge,
    w_gate,
    w_coord,
    w_weight,
    w_node,
    a_out,
    w2_out,
    w3_out,
    ww_out,
    place_out,
    node_out,
):
    rows, width = feat.shape
    x = feat[...]
    tgt = (dot(x, w_tgt[...]) + edge_bias[...]) * 0.5
    tgt_hi, tgt_lo = split2(tgt)
    dist = w_dist[...] * 0.5
    d_hi = dist.astype(BF16).astype(F32)
    d_lo = dist - d_hi
    row = lax.broadcasted_iota(jnp.int32, (16, width), 0)
    tail = jnp.where(row == 1, d_lo, jnp.where(row < 3, d_hi, 0.0)).astype(BF16)
    half = jnp.asarray(0.5, BF16)
    stacked = jnp.concatenate([w_src[...] * half, tgt_hi, tgt_lo, tail], axis=0)
    a_out[...] = stacked.T
    w2_out[...] = (w_edge[...] * half).T
    gate = w_gate[...]
    g_hi = gate.astype(BF16).astype(F32)
    g_rows = jnp.where(row == 0, g_hi, jnp.where(row == 1, gate - g_hi, 0.0)).astype(BF16)
    w3_out[...] = jnp.concatenate([(w_coord[...] * half).T, g_rows], axis=0)
    ww_out[...] = jnp.broadcast_to(w_weight[...], (LANES, width)).T
    own = jnp.concatenate([coords[...].astype(F32), jnp.zeros((5, rows), F32)], axis=0)
    own = jnp.concatenate([own, jnp.zeros((8, LANES - rows), F32)], axis=1)
    col = own.T
    for c in range(3):
        place_out[c] = jnp.broadcast_to(col[:rows, c : c + 1], (rows, LANES))
    node_out[...] = dot(x, w_node[:width, :])


def edge_body(
    where,
    table,
    far,
    a_ref,
    w2_ref,
    w3_ref,
    ww_ref,
    place_ref,
    node_ref,
    feat,
    coords,
    w_node,
    w_out,
    feat_out,
    coord_out,
    *,
    edge_parts,
    mean_scale,
):
    rows, width = feat.shape
    rounds = table.shape[0]
    block = where[0]
    part = where[1]
    homes = [block] + [table[r, block] for r in range(rounds)]
    pieces = [far[h * edge_parts + e] for h in homes for e in range(edge_parts)]
    sources = rows * len(pieces)
    parts = sources // LANES
    src = jnp.concatenate([p[:rows] for p in pieces], axis=0)
    src_t = src.T
    spots = jnp.concatenate([p[rows:].astype(F32)[:, :rows] for p in pieces], axis=1)
    lane = lax.broadcasted_iota(jnp.int32, (rows, LANES), 1)
    trow = lax.broadcasted_iota(jnp.int32, (rows, LANES), 0)
    offs, radial, unit, keep, r_hi, r_lo = [], [], [], [], [], []
    for q in range(parts):
        cut = slice(q * LANES, (q + 1) * LANES)
        off = [place_ref[c] - spots[c : c + 1, cut] for c in range(3)]
        rad = off[0] * off[0] + off[1] * off[1] + off[2] * off[2]
        scale = 1.0 / (jnp.sqrt(rad) + 1.0)
        unit.append([o * scale for o in off])
        keep.append(jnp.where(lane + q * LANES == part * rows + trow, 0.0, 1.0))
        hi = rad.astype(BF16).astype(F32)
        r_hi.append(hi)
        r_lo.append(rad - hi)
    a = a_ref[...]
    w2 = w2_ref[...]
    w3 = w3_ref[...]
    urow = lax.broadcasted_iota(jnp.int32, (16, LANES), 0)
    pairs = [(i, q) for i in range(rows) for q in range(parts)]
    group = 2 if len(pairs) % 2 == 0 else 1
    total = jnp.zeros((2 * rows, width), F32)
    weight_rows = {}
    for at in range(0, len(pairs), group):
        members = pairs[at : at + group]
        right = []
        for i, q in members:
            pick = jnp.where(trow == i, 1.0, 0.0).astype(BF16)
            tail = jnp.where(
                urow < 2, r_hi[q][i : i + 1], jnp.where(urow == 2, r_lo[q][i : i + 1], 0.0)
            ).astype(BF16)
            right.append(
                jnp.concatenate(
                    [src_t[:, q * LANES : (q + 1) * LANES], pick, pick, tail], axis=0
                )
            )
        hidden = half_silu(dot(a, jnp.concatenate(right, axis=1))).astype(BF16)
        low = half_silu(dot(w2, hidden)).astype(BF16)
        lifted = dot(w3, low)
        gate = jax.nn.sigmoid(lifted[width : width + 1] + lifted[width + 1 : width + 2])
        lifted = half_silu(lifted[:width])
        left = []
        for m, (i, q) in enumerate(members):
            cut = slice(m * LANES, (m + 1) * LANES)
            weight_rows[i, q] = jnp.sum(lifted[:, cut] * ww_ref[...], axis=0, keepdims=True)
            g = jnp.where(trow == i, gate[:, cut] * keep[q], 0.0)
            left.append(jnp.concatenate(split2(g), axis=0))
        left = jnp.concatenate(left, axis=1)
        total = total + lax.dot_general(
            left, low, (((1,), (1,)), ((), ())), preferred_element_type=F32
        )
    message_mean = ((total[:rows] + total[rows:]) * mean_scale).astype(BF16)
    node_pre = node_ref[...] + dot(message_mean, w_node[width:, :])
    node_hidden = half_silu(node_pre * 0.5).astype(BF16)
    feat_out[...] = (feat[...].astype(F32) + dot(node_hidden, w_out[...])).astype(BF16)
    sums = [jnp.zeros((rows, 1), F32)] * 3
    for q in range(parts):
        weight = jnp.concatenate([weight_rows[i, q] for i in range(rows)], axis=0) * keep[q]
        for c in range(3):
            sums[c] = sums[c] + jnp.sum(unit[q][c] * weight, axis=1, keepdims=True)
    table_cols = jnp.where(lane == 0, sums[0], jnp.where(lane == 1, sums[1], sums[2]))
    coord_out[...] = coords[...].astype(F32) + table_cols.T[:3] * mean_scale


def shards(
    node_feat,
    coords,
    pair_table,
    w_tgt,
    w_src,
    w_dist,
    edge_bias,
    w_edge,
    w_gate,
    w_coord,
    w_weight,
    w_node_in,
    w_node_out,
):
    rows, width = node_feat.shape
    edge_parts = lax.axis_size("edge")
    devices = lax.axis_size("blk") * edge_parts
    rounds = pair_table.shape[0]
    mean_scale = 1.0 / ((rounds + 1) * rows * edge_parts - 1)
    spot = jnp.pad(coords, ((0, 5), (0, width - rows)))
    pack = jnp.concatenate([node_feat, spot], axis=0)
    sent = jnp.broadcast_to(pack[None], (devices,) + pack.shape)
    far = lax.all_to_all(sent, ("blk", "edge"), 0, 0, tiled=True)
    where = jnp.stack([lax.axis_index("blk"), lax.axis_index("edge")]).astype(jnp.int32)
    line = lambda v: v.reshape(1, -1)
    vmem = pl.BlockSpec(memory_space=pltpu.VMEM)
    smem = pl.BlockSpec(memory_space=pltpu.SMEM)
    depth = width + 2 * rows + 16
    prepared = pl.pallas_call(
        prep_body,
        out_shape=(
            jax.ShapeDtypeStruct((width, depth), BF16),
            jax.ShapeDtypeStruct((width, width), BF16),
            jax.ShapeDtypeStruct((width + 16, width), BF16),
            jax.ShapeDtypeStruct((width, LANES), F32),
            jax.ShapeDtypeStruct((3, rows, LANES), F32),
            jax.ShapeDtypeStruct((rows, width), F32),
        ),
        in_specs=[vmem] * 11,
        out_specs=(vmem,) * 6,
        name="prepare",
    )(
        node_feat,
        coords,
        w_tgt,
        w_src,
        line(w_dist),
        line(edge_bias),
        w_edge,
        line(w_gate),
        w_coord,
        line(w_weight),
        w_node_in,
    )

    def body(*refs):
        edge_body(*refs, edge_parts=edge_parts, mean_scale=mean_scale)

    return pl.pallas_call(
        body,
        out_shape=(
            jax.ShapeDtypeStruct((rows, width), BF16),
            jax.ShapeDtypeStruct((3, rows), F32),
        ),
        in_specs=[smem, smem] + [vmem] * 11,
        out_specs=(vmem, vmem),
        name="edges",
    )(where, pair_table, far, *prepared, node_feat, coords, w_node_in, w_node_out)


def solution(mesh):
    whole = P()
    placed = (P(("blk", "edge"), None), P(None, ("blk", "edge"))) + (whole,) * 11
    return jax.shard_map(
        shards,
        mesh=mesh,
        in_specs=placed,
        out_specs=(P(("blk", "edge"), None), P(None, ("blk", "edge"))),
        check_vma=False,
    )
```

time: 131 us -> 24.1 us (0.18)
  blocking collectives: 81.9 us -> 0 us
  between operations: 20.3 us -> 0.65 us
  starting transfers between devices: 0.08 us -> 7.33 us
  Pallas kernels: 0 us -> 6.67 us
  waiting for transfers between devices: 12.9 us -> 6.38 us
  local copies, waits for them, and re-layouts: 7.69 us -> 1.37 us
  matrix products: 4.56 us -> 0 us
  other arithmetic: 2.76 us -> 1.38 us
    all_gather x4 -> x0, blocking collectives: 81.9 us -> none  [the longest x1 42.7 us: shards(): lax.all_gather(node_feat[None], 'blk', axis=0, tiled=True)]
    reduce_scatter x1 -> x0, waiting for transfers between devices: 9.48 us -> none  [shards(): lax.psum_scatter(message_sum, 'edge', scatter_dimension=0, tiled=True)]
    all_to_all x0 -> x1, starting transfers between devices: none -> 7.33 us  [shards(): far = lax.all_to_all(sent, ('blk', 'edge'), 0, 0, tiled=True)]
    pallas_call x0 -> x2, Pallas kernels: none -> 6.67 us  [the longest x1 4.77 us: shards(): pl.pallas_call(body, out_shape=(jax.ShapeDtypeStruct((rows, width), BF16)...]
    all_to_all x0 -> x1, waiting for transfers between devices: none -> 6.38 us  [shards(): far = lax.all_to_all(sent, ('blk', 'edge'), 0, 0, tiled=True)]
    unnamed x28 -> x2, local copies, waits for them, and re-layouts: 5.39 us -> 0.67 us
    dot_general x15 -> x0, matrix products: 4.56 us -> none  [the longest x1 1.55 us: shards(): jnp.dot(node_hidden, w_node_out, preferred_element_type=jnp.float32)]
    unnamed x3 -> x0, waiting for transfers between devices: 3.42 us -> none
  transfers between devices with their start and end apart: 2 -> 1, of which waited for: 2 -> 1; matrix products, arithmetic and copies ran while one was open for 2% -> 3% of each run, Pallas kernels for 0% -> 8%
where the time goes in v1:
time: 24.1 us; the launch traced here: 23.8 us
  starting transfers between devices  7.33 us (30%)
  Pallas kernels  6.67 us (28%)
  waiting for transfers between devices  6.38 us (26%)
  other arithmetic  1.38 us (6%)
  local copies, waits for them, and re-layouts  1.37 us (6%)
  between operations  0.65 us (3%)
    all_to_all x1, starting transfers between devices, shards(): far = lax.all_to_all(sent, ('blk', 'edge'), 0, 0, tiled=True)  7.33 us
    all_to_all x1, waiting for transfers between devices, shards(): far = lax.all_to_all(sent, ('blk', 'edge'), 0, 0, tiled=True)  6.38 us
    pallas_call x1, Pallas kernels, shards(): pl.pallas_call(body, out_shape=(jax.ShapeDtypeStruct((rows, width), BF16)...  4.77 us
    pallas_call x1, Pallas kernels, shards(): pl.pallas_call(prep_body, out_shape=(jax.ShapeDtypeStruct((width, depth),...  1.9 us
    concatenate x1, other arithmetic, shards(): pack = jnp.concatenate([node_feat, spot], axis=0)  0.71 us
    broadcast_in_dim x1, local copies, waits for them, and re-layouts, shards(): sent = jnp.broadcast_to(pack[None], (devices,) + pack.shape)  0.7 us
    unnamed x2, local copies, waits for them, and re-layouts  0.67 us
    another operation x1, other arithmetic, shards(): jnp.stack([lax.axis_index('blk'), lax.axis_index('edge')]).astype(jnp.int32)  0.67 us
  transfers between devices with their start and end apart: 1, of which 1 were waited for; matrix products, arithmetic and copies ran while one was open for 3% of the time, Pallas kernels for 8%

profile of v1, /device:TPU:0, one launch (start us, length us, event | category | flops | bytes accessed | tf_op | source)
XLA Modules:
  0.0 23.8 jit_solution(241194123880876022)
XLA Ops:
  0.6 0.7 %fusion.1 = bf16[24,128]{1,0:T(8,128)(2,1)S(1)} fusion(bf16[3,16]{1,0:T(4,128)(2,1)} %refs_10_.1, bf16[16,128]{1,0:T(8,128)(2,1)} %refs_9_.1), kind=kLoop, calls=%fused_computation.2 | loop fusion | flops 18432 | bytes 10336 | tf_op jit(solution)/shard_map/concatenate | solution.py:186
  1.3 0.7 %broadcast_in_dim.2 = bf16[32,24,128]{2,1,0:T(8,128)(2,1)} broadcast(bf16[24,128]{1,0:T(8,128)(2,1)S(1)} %fusion.1), dimensions={1,2} | broadcast | bytes 202752 | tf_op jit(solution)/shard_map/broadcast_in_dim | solution.py:187
  2.0 7.3 %all-to-all-start = ((bf16[32,24,128]{2,1,0:T(8,128)(2,1)}), bf16[32,24,128]{2,1,0:T(8,128)(2,1)S(1)}, u32[]{:S(2)}, u32[]{:S(2)}) async-start(bf16[32,24,128]{2,1,0:T(8,128)(2,1)} %broadcast_in_dim.2), calls=%async_computation | async-start | bytes 393216 | tf_op jit(solution)/shard_map/all_to_all | solution.py:188
  9.4 1.9 %prepare.1 = (bf16[128,176]{1,0:T(8,128)(2,1)}, bf16[128,128]{1,0:T(8,128)(2,1)}, bf16[144,128]{1,0:T(8,128)(2,1)}, f32[128,128]{1,0:T(8,128)}, f32[3,16,128]{2,1,0:T(8,128)}, /*index=5*/f32[16,128]{1,0:T(8,128)}) custom-call(bf16[16,128]{1,0:T(8,128)(2,1)} %refs_9_.1, bf16[3,16]{1,0:T(4,128)(2,1)} %refs_10_.1, bf16[128,128]{1,0:T(8,128)(2,1)} %w_tgt.1, ...), custom_call_target="tpu_custom_call" | custom-call | tf_op jit(solution)/shard_map/prepare/pallas_call | solution.py:194
  11.3 0.7 %pad_add_fusion.refs_0_ = s32[2]{0:T(128)} fusion(s32[1]{0:T(128)} %bitcast.1, s32[1]{0:T(128)} %bitcast), kind=kLoop, calls=%fused_computation.3 | loop fusion | flops 2 | bytes 16 | tf_op jit(solution)/shard_map/stack | solution.py:189
  11.9 6.4 %all-to-all-done.refs_2_ = bf16[32,24,128]{2,1,0:T(8,128)(2,1)S(1)} async-done(((bf16[32,24,128]{2,1,0:T(8,128)(2,1)}), bf16[32,24,128]{2,1,0:T(8,128)(2,1)S(1)}, u32[]{:S(2)}, u32[]{:S(2)}) %all-to-all-start) | async-done | bytes 196640 | tf_op jit(solution)/shard_map/all_to_all | solution.py:188
  18.3 0.0 copy-start
  18.3 0.7 %copy-done = bf16[32,24,128]{2,1,0:T(8,128)(2,1)} copy-done((bf16[32,24,128]{2,1,0:T(8,128)(2,1)}, bf16[32,24,128]{2,1,0:T(8,128)(2,1)S(1)}, u32[]{:S(2)}) %copy-start) | copy-done | bytes 196632
  19.0 4.8 %edges.1 = (bf16[16,128]{1,0:T(8,128)(2,1)}, f32[3,16]{1,0:T(4,128)}) custom-call(s32[2]{0:T(128)} %pad_add_fusion.refs_0_, s32[3,16]{1,0:T(4,128)} %refs_1_.1, bf16[32,24,128]{2,1,0:T(8,128)(2,1)} %copy-done, bf16[128,176]{1,0:T(8,128)(2,1)} %get-tuple-element.8.refs_3_, bf16[128,128]{1,0:T(8,128)(2,1)} %get-tuple-element.9.refs_4_, ...), custom_call_target="tpu_custom_call" | custom-call | tf_op jit(solution)/shard_map/edges/pallas_call | solution.py:224
Async XLA Ops:
  2.0 16.3 %all-to-all-start = ((bf16[32,24,128]{2,1,0:T(8,128)(2,1)}), bf16[32,24,128]{2,1,0:T(8,128)(2,1)S(1)}, u32[]{:S(2)}, u32[]{:S(2)}) async-start(bf16[32,24,128]{2,1,0:T(8,128)(2,1)} %broadcast_in_dim.2), calls=%async_computation | async-start | bytes 393216 | tf_op jit(solution)/shard_map/all_to_all | solution.py:188
  18.3 0.7 %copy-start = (bf16[32,24,128]{2,1,0:T(8,128)(2,1)}, bf16[32,24,128]{2,1,0:T(8,128)(2,1)S(1)}, u32[]{:S(2)}) copy-start(bf16[32,24,128]{2,1,0:T(8,128)(2,1)S(1)} %all-to-all-done.refs_2_) | copy-start | bytes 589828

commit v2 on v1

v2 whole, which is shorter than its diff:
```python
import jax
import jax.numpy as jnp
from jax import lax
from jax.experimental import pallas as pl
from jax.experimental.pallas import tpu as pltpu
from jax.sharding import PartitionSpec as P

F32 = jnp.float32
BF16 = jnp.bfloat16
LANES = 128
VMEM_BYTES = 24 * 2**20
WAVE = 8


def split2(x):
    hi = x.astype(BF16)
    lo = (x - hi.astype(F32)).astype(BF16)
    return hi, lo


def dot(a, b):
    return jnp.dot(a, b, preferred_element_type=F32)


def half_silu(h):
    return h + h * jnp.tanh(h)


def pack_body(feat, coords, table, w_dist, edge_bias, w_gate, w_weight, sent, lines, table_out):
    rows, width = feat.shape
    spot = jnp.concatenate([coords[...].astype(F32), jnp.zeros((5, rows), F32)], axis=0)
    spot = jnp.concatenate([spot, jnp.zeros((8, width - rows), F32)], axis=1)
    one = jnp.concatenate([feat[...], spot.astype(BF16)], axis=0)
    sent[...] = jnp.broadcast_to(one[None], sent.shape)
    for k, line in enumerate((w_dist, edge_bias, w_gate, w_weight)):
        lines[k : k + 1, :] = line[...]
    for r in range(table.shape[0]):
        for b in range(table.shape[1]):
            table_out[r, b] = table[r, b]


def edge_body(
    table,
    far,
    lines,
    w_tgt,
    w_src,
    w_edge,
    w_coord,
    w_node,
    w_out,
    feat_out,
    coord_out,
    *,
    edge_parts,
    mean_scale,
):
    rows, width = feat_out.shape
    rounds = table.shape[0]
    block = lax.axis_index("blk")
    part = lax.axis_index("edge")
    blocks = [block] + [table[r, block] for r in range(rounds)]
    pieces = [far[h * edge_parts + e] for h in blocks for e in range(edge_parts)]
    parts = rows * len(pieces) // LANES
    half = jnp.asarray(0.5, BF16)

    src_t = jnp.concatenate([p[:rows] for p in pieces], axis=0).T
    spots = jnp.concatenate([p[rows:].astype(F32)[:, :rows] for p in pieces], axis=1)

    own = far[block * edge_parts + part]
    x = own[:rows]
    w_dist, edge_bias, w_gate, w_weight = (lines[k : k + 1, :] for k in range(4))
    tgt_hi, tgt_lo = split2((dot(x, w_tgt[...]) + edge_bias) * 0.5)
    dist = w_dist * 0.5
    d_hi = dist.astype(BF16).astype(F32)
    urow = lax.broadcasted_iota(jnp.int32, (16, width), 0)
    tail = jnp.where(urow == 1, dist - d_hi, jnp.where(urow < 3, d_hi, 0.0)).astype(BF16)
    a = jnp.concatenate([w_src[...] * half, tgt_hi, tgt_lo, tail], axis=0).T
    w2 = (w_edge[...] * half).T
    gate_w = w_gate
    g_hi = gate_w.astype(BF16).astype(F32)
    g_rows = jnp.where(urow == 0, g_hi, jnp.where(urow == 1, gate_w - g_hi, 0.0)).astype(BF16)
    w3 = jnp.concatenate([(w_coord[...] * half).T, g_rows], axis=0)
    ww = jnp.broadcast_to(w_weight, (LANES, width)).T
    spot = own[rows:].astype(F32)
    col = spot.T[:rows]
    node_part = dot(x, w_node[:width, :])

    lane = lax.broadcasted_iota(jnp.int32, (rows, LANES), 1)
    trow = lax.broadcasted_iota(jnp.int32, (rows, LANES), 0)
    unit, keep, r_hi, r_lo = [], [], [], []
    for q in range(parts):
        cut = slice(q * LANES, (q + 1) * LANES)
        off = [col[:, c : c + 1] - spots[c : c + 1, cut] for c in range(3)]
        rad = off[0] * off[0] + off[1] * off[1] + off[2] * off[2]
        scale = 1.0 / (jnp.sqrt(rad) + 1.0)
        unit.append([o * scale for o in off])
        keep.append(jnp.where(lane + q * LANES == part * rows + trow, 0.0, 1.0))
        hi = rad.astype(BF16).astype(F32)
        r_hi.append(hi)
        r_lo.append(rad - hi)
    lrow = lax.broadcasted_iota(jnp.int32, (16, LANES), 0)
    pairs = [(i, q) for i in range(rows) for q in range(parts)]
    group = 2 if len(pairs) % 2 == 0 else 1
    chunks = [pairs[at : at + group] for at in range(0, len(pairs), group)]
    rights = []
    for members in chunks:
        right = []
        for i, q in members:
            pick = jnp.where(trow == i, 1.0, 0.0).astype(BF16)
            near = jnp.where(
                lrow < 2, r_hi[q][i : i + 1], jnp.where(lrow == 2, r_lo[q][i : i + 1], 0.0)
            ).astype(BF16)
            here = src_t[:, q * LANES : (q + 1) * LANES]
            right.append(jnp.concatenate([here, pick, pick, near], axis=0))
        rights.append(jnp.concatenate(right, axis=1))
    wave = WAVE
    total = jnp.zeros((2 * rows, width), F32)
    weight_rows = {}
    for at in range(0, len(chunks), wave):
        now = range(at, min(at + wave, len(chunks)))
        hidden = [dot(a, rights[k]) for k in now]
        hidden = [half_silu(h).astype(BF16) for h in hidden]
        low = [dot(w2, h) for h in hidden]
        low = [half_silu(h).astype(BF16) for h in low]
        lifted = [dot(w3, h) for h in low]
        gates = [jax.nn.sigmoid(v[width : width + 1] + v[width + 1 : width + 2]) for v in lifted]
        for k, g, m in zip(now, gates, low):
            left = []
            for n, (i, q) in enumerate(chunks[k]):
                cut = slice(n * LANES, (n + 1) * LANES)
                kept = jnp.where(trow == i, g[:, cut] * keep[q], 0.0)
                left.append(jnp.concatenate(split2(kept), axis=0))
            total = total + lax.dot_general(
                jnp.concatenate(left, axis=1),
                m,
                (((1,), (1,)), ((), ())),
                preferred_element_type=F32,
            )
        for k, v in zip(now, lifted):
            v = half_silu(v[:width])
            for n, (i, q) in enumerate(chunks[k]):
                cut = slice(n * LANES, (n + 1) * LANES)
                weight_rows[i, q] = jnp.sum(v[:, cut] * ww, axis=0, keepdims=True)
    message_mean = ((total[:rows] + total[rows:]) * mean_scale).astype(BF16)
    node_pre = node_part + dot(message_mean, w_node[width:, :])
    node_hidden = half_silu(node_pre * 0.5).astype(BF16)
    feat_out[...] = (x.astype(F32) + dot(node_hidden, w_out[...])).astype(BF16)
    sums = [jnp.zeros((rows, 1), F32)] * 3
    for q in range(parts):
        weight = jnp.concatenate([weight_rows[i, q] for i in range(rows)], axis=0) * keep[q]
        for c in range(3):
            sums[c] = sums[c] + jnp.sum(unit[q][c] * weight, axis=1, keepdims=True)
    side = jnp.where(lane == 0, sums[0], jnp.where(lane == 1, sums[1], sums[2]))
    coord_out[...] = spot[:3, :rows] + side.T[:3] * mean_scale


def shards(
    node_feat,
    coords,
    pair_table,
    w_tgt,
    w_src,
    w_dist,
    edge_bias,
    w_edge,
    w_gate,
    w_coord,
    w_weight,
    w_node_in,
    w_node_out,
):
    rows, width = node_feat.shape
    edge_parts = lax.axis_size("edge")
    devices = lax.axis_size("blk") * edge_parts
    rounds = pair_table.shape[0]
    mean_scale = 1.0 / ((rounds + 1) * rows * edge_parts - 1)
    vmem = pl.BlockSpec(memory_space=pltpu.VMEM)
    smem = pl.BlockSpec(memory_space=pltpu.SMEM)
    params = pltpu.CompilerParams(vmem_limit_bytes=VMEM_BYTES)
    line = lambda v: v.reshape(1, -1)
    small = (line(w_dist), line(edge_bias), line(w_gate), line(w_weight))
    hold = lambda v: pltpu.with_memory_space_constraint(v, pltpu.HBM)
    sent, lines, table = pl.pallas_call(
        pack_body,
        out_shape=(
            pltpu.VMEM((devices, rows + 8, width), BF16),
            pltpu.VMEM((8, width), F32),
            pltpu.SMEM(pair_table.shape, pair_table.dtype),
        ),
        in_specs=[vmem] * 2 + [smem] + [vmem] * 4,
        out_specs=(vmem, vmem, smem),
        compiler_params=params,
        name="pack",
    )(*(hold(v) for v in (node_feat, coords, pair_table) + small))
    far = lax.all_to_all(sent, ("blk", "edge"), 0, 0, tiled=True)

    def body(*refs):
        edge_body(*refs, edge_parts=edge_parts, mean_scale=mean_scale)

    return pl.pallas_call(
        body,
        out_shape=(
            jax.ShapeDtypeStruct((rows, width), BF16),
            jax.ShapeDtypeStruct((3, rows), F32),
        ),
        in_specs=[smem] + [vmem] * 8,
        out_specs=(vmem, vmem),
        compiler_params=params,
        name="edges",
    )(
        table,
        far,
        lines,
        w_tgt,
        w_src,
        w_edge,
        w_coord,
        w_node_in,
        w_node_out,
    )


def solution(mesh):
    whole = P()
    placed = (P(("blk", "edge"), None), P(None, ("blk", "edge"))) + (whole,) * 11
    return jax.shard_map(
        shards,
        mesh=mesh,
        in_specs=placed,
        out_specs=(P(("blk", "edge"), None), P(None, ("blk", "edge"))),
        check_vma=False,
    )
```

time: 24.1 us -> 20 us (0.83)
  blocking collectives: 0 us -> 16.1 us
  starting transfers between devices: 7.33 us -> 0 us
  waiting for transfers between devices: 6.38 us -> 0 us
  Pallas kernels: 6.67 us -> 2.91 us
  other arithmetic: 1.38 us -> 0 us
  local copies, waits for them, and re-layouts: 1.37 us -> 0.04 us
    all_to_all x0 -> x1, blocking collectives: none -> 16.1 us  [shards(): far = lax.all_to_all(sent, ('blk', 'edge'), 0, 0, tiled=True)]
    all_to_all x1 -> x0, starting transfers between devices: 7.33 us -> none  [shards(): far = lax.all_to_all(sent, ('blk', 'edge'), 0, 0, tiled=True)]
    all_to_all x1 -> x0, waiting for transfers between devices: 6.38 us -> none  [shards(): far = lax.all_to_all(sent, ('blk', 'edge'), 0, 0, tiled=True)]
    pallas_call x1, Pallas kernels: 4.77 us -> 2.03 us  [shards(): pl.pallas_call(body, out_shape=(jax.ShapeDtypeStruct((rows, width), BF16)...]
    pallas_call x1, Pallas kernels: 1.9 us -> 0.88 us  [shards(): pl.pallas_call(pack_body, out_shape=(pltpu.VMEM((devices, rows + 8, width...]
    concatenate x1 -> x0, other arithmetic: 0.71 us -> none  [shards(): pack = jnp.concatenate([node_feat, spot], axis=0)]
    broadcast_in_dim x1 -> x0, local copies, waits for them, and re-layouts: 0.7 us -> none  [shards(): sent = jnp.broadcast_to(pack[None], (devices,) + pack.shape)]
    another operation x1 -> x0, other arithmetic: 0.67 us -> none  [shards(): jnp.stack([lax.axis_index('blk'), lax.axis_index('edge')]).astype(jnp.int32)]
  transfers between devices with their start and end apart: 1 -> 0, of which waited for: 1 -> 0; matrix products, arithmetic and copies ran while one was open for 3% -> 0% of each run, Pallas kernels for 8% -> 0%
where the time goes in v2:
time: 20 us; the launch traced here: 19.7 us
  blocking collectives  16.1 us (81%)
  Pallas kernels  2.91 us (15%)
  between operations  0.72 us (4%)
    all_to_all x1, blocking collectives, shards(): far = lax.all_to_all(sent, ('blk', 'edge'), 0, 0, tiled=True)  16.1 us
    pallas_call x1, Pallas kernels, shards(): pl.pallas_call(body, out_shape=(jax.ShapeDtypeStruct((rows, width), BF16)...  2.03 us
    pallas_call x1, Pallas kernels, shards(): pl.pallas_call(pack_body, out_shape=(pltpu.VMEM((devices, rows + 8, width...  0.88 us

profile of v2, /device:TPU:0, one launch (start us, length us, event | category | flops | bytes accessed | tf_op | source)
XLA Modules:
  0.0 19.7 jit_solution(3654009876582005570)
XLA Ops:
  0.6 0.9 %pack.1 = (bf16[32,24,128]{2,1,0:T(8,128)(2,1)S(1)}, f32[8,128]{1,0:T(8,128)S(1)}, s32[3,16]{1,0:T(4,128)S(4)}) custom-call(bf16[16,128]{1,0:T(8,128)(2,1)} %feat.1, bf16[3,16]{1,0:T(4,128)(2,1)} %coords.1, s32[3,16]{1,0:T(4,128)} %table.1, f32[1,128]{1,0:T(1,128)} %bitcast.4, f32[1,128]{1,0:T(1,128)} %bitcast.5, f32[1,128]{1,0:T(1,128)} %bitcast.6, ...), custom_call_target="tpu_custom_call" | custom-call | tf_op jit(solution)/shard_map/pack/pallas_call | solution.py:184
  1.5 0.0 copy-start
  1.5 0.0 copy-start.1
  1.5 0.0 copy-start.2
  1.6 0.0 copy-start.3
  1.6 0.0 copy-start.4
  1.6 0.0 copy-start.5
  1.6 16.1 %all_to_all.5.refs_1_ = bf16[32,24,128]{2,1,0:T(8,128)(2,1)S(1)} all-to-all(bf16[32,24,128]{2,1,0:T(8,128)(2,1)S(1)} %get-tuple-element.6), channel_id=1, replica_groups=mesh['blk'=16,'edge'=2] {'blk','edge'}, dimensions={0} | all-to-all | bytes 393216 | tf_op jit(solution)/shard_map/all_to_all | solution.py:196
  17.7 0.0 copy-done
  17.7 0.0 copy-done.1
  17.7 0.0 copy-done.2
  17.7 0.0 copy-done.3
  17.7 0.0 copy-done.4
  17.7 0.0 copy-done.5
  17.7 2.0 %edges.1 = (bf16[16,128]{1,0:T(8,128)(2,1)}, f32[3,16]{1,0:T(4,128)}) custom-call(s32[3,16]{1,0:T(4,128)S(4)} %get-tuple-element.5.refs_0_, bf16[32,24,128]{2,1,0:T(8,128)(2,1)S(1)} %all_to_all.5.refs_1_, f32[8,128]{1,0:T(8,128)S(1)} %get-tuple-element.7.refs_2_, bf16[128,128]{1,0:T(8,128)(2,1)S(1)} %copy-done.1, bf16[128,128]{1,0:T(8,128)(2,1)S(1)} %copy-done.2, ...), custom_call_target="tpu_custom_call" | custom-call | tf_op jit(solution)/shard_map/edges/pallas_call | solution.py:201
Async XLA Ops:
  1.5 16.2 %copy-start = (bf16[256,128]{1,0:T(8,128)(2,1)S(1)}, bf16[256,128]{1,0:T(8,128)(2,1)}, u32[]{:S(2)}) copy-start(bf16[256,128]{1,0:T(8,128)(2,1)} %refs_7_.1) | copy-start | bytes 196612
  1.5 16.1 %copy-start.1 = (bf16[128,128]{1,0:T(8,128)(2,1)S(1)}, bf16[128,128]{1,0:T(8,128)(2,1)}, u32[]{:S(2)}) copy-start(bf16[128,128]{1,0:T(8,128)(2,1)} %refs_3_.1) | copy-start | bytes 98308
  1.5 16.1 %copy-start.2 = (bf16[128,128]{1,0:T(8,128)(2,1)S(1)}, bf16[128,128]{1,0:T(8,128)(2,1)}, u32[]{:S(2)}) copy-start(bf16[128,128]{1,0:T(8,128)(2,1)} %refs_4_.1) | copy-start | bytes 98308
  1.6 16.1 %copy-start.3 = (bf16[128,128]{1,0:T(8,128)(2,1)S(1)}, bf16[128,128]{1,0:T(8,128)(2,1)}, u32[]{:S(2)}) copy-start(bf16[128,128]{1,0:T(8,128)(2,1)} %refs_5_.1) | copy-start | bytes 98308
  1.6 16.1 %copy-start.4 = (bf16[128,128]{1,0:T(8,128)(2,1)S(1)}, bf16[128,128]{1,0:T(8,128)(2,1)}, u32[]{:S(2)}) copy-start(bf16[128,128]{1,0:T(8,128)(2,1)} %refs_6_.1) | copy-start | bytes 98308
  1.6 16.1 %copy-start.5 = (bf16[128,128]{1,0:T(8,128)(2,1)S(1)}, bf16[128,128]{1,0:T(8,128)(2,1)}, u32[]{:S(2)}) copy-start(bf16[128,128]{1,0:T(8,128)(2,1)} %refs_8_.1) | copy-start | bytes 98308

commit v3 on v2

--- a/solution.py
+++ b/solution.py
@@ -9,7 +9,8 @@
 BF16 = jnp.bfloat16
 LANES = 128
 VMEM_BYTES = 24 * 2**20
-WAVE = 8
+SPLIT = 2
+SLAB = 4
 
 
 def split2(x):
@@ -28,10 +29,11 @@
 
 def pack_body(feat, coords, table, w_dist, edge_bias, w_gate, w_weight, sent, lines, table_out):
     rows, width = feat.shape
-    spot = jnp.concatenate([coords[...].astype(F32), jnp.zeros((5, rows), F32)], axis=0)
-    spot = jnp.concatenate([spot, jnp.zeros((8, width - rows), F32)], axis=1)
-    one = jnp.concatenate([feat[...], spot.astype(BF16)], axis=0)
-    sent[...] = jnp.broadcast_to(one[None], sent.shape)
+    spot = jnp.concatenate([coords[...].astype(F32), jnp.zeros((SLAB - 3, rows), F32)], axis=0)
+    spot = jnp.concatenate([spot, jnp.zeros((SLAB, width - rows), F32)], axis=1)
+    slabs = [feat[k : k + SLAB, :] for k in range(0, rows, SLAB)] + [spot.astype(BF16)]
+    for k, slab in enumerate(slabs):
+        sent[:, k] = jnp.broadcast_to(slab[None], (sent.shape[0],) + slab.shape)
     for k, line in enumerate((w_dist, edge_bias, w_gate, w_weight)):
         lines[k : k + 1, :] = line[...]
     for r in range(table.shape[0]):
@@ -60,29 +62,38 @@
     block = lax.axis_index("blk")
     part = lax.axis_index("edge")
     blocks = [block] + [table[r, block] for r in range(rounds)]
-    pieces = [far[h * edge_parts + e] for h in blocks for e in range(edge_parts)]
-    parts = rows * len(pieces) // LANES
+    places = [h * edge_parts + e for h in blocks for e in range(edge_parts)]
+    slabs = rows // SLAB
+
+    def feats(p):
+        return [far[p, k] for k in range(slabs)]
+
+    def spots_of(p):
+        return far[p, slabs].astype(F32)
+
+    parts = rows * len(places) // LANES
     half = jnp.asarray(0.5, BF16)
 
-    src_t = jnp.concatenate([p[:rows] for p in pieces], axis=0).T
-    spots = jnp.concatenate([p[rows:].astype(F32)[:, :rows] for p in pieces], axis=1)
-
-    own = far[block * edge_parts + part]
-    x = own[:rows]
+    src_t = jnp.concatenate([f for p in places for f in feats(p)], axis=0).T
+    spots = jnp.concatenate([spots_of(p)[:, :rows] for p in places], axis=1)
+
+    own = block * edge_parts + part
+    x = jnp.concatenate(feats(own), axis=0)
     w_dist, edge_bias, w_gate, w_weight = (lines[k : k + 1, :] for k in range(4))
     tgt_hi, tgt_lo = split2((dot(x, w_tgt[...]) + edge_bias) * 0.5)
     dist = w_dist * 0.5
     d_hi = dist.astype(BF16).astype(F32)
     urow = lax.broadcasted_iota(jnp.int32, (16, width), 0)
     tail = jnp.where(urow == 1, dist - d_hi, jnp.where(urow < 3, d_hi, 0.0)).astype(BF16)
-    a = jnp.concatenate([w_src[...] * half, tgt_hi, tgt_lo, tail], axis=0).T
+    a = jnp.concatenate([tgt_hi, tgt_lo, tail], axis=0).T
+    src_proj = dot((w_src[...] * half).T, src_t)
     w2 = (w_edge[...] * half).T
     gate_w = w_gate
     g_hi = gate_w.astype(BF16).astype(F32)
     g_rows = jnp.where(urow == 0, g_hi, jnp.where(urow == 1, gate_w - g_hi, 0.0)).astype(BF16)
     w3 = jnp.concatenate([(w_coord[...] * half).T, g_rows], axis=0)
     ww = jnp.broadcast_to(w_weight, (LANES, width)).T
-    spot = own[rows:].astype(F32)
+    spot = jnp.concatenate([spots_of(own), jnp.zeros((8 - SLAB, width), F32)], axis=0)
     col = spot.T[:rows]
     node_part = dot(x, w_node[:width, :])
 
@@ -111,41 +122,47 @@
             near = jnp.where(
                 lrow < 2, r_hi[q][i : i + 1], jnp.where(lrow == 2, r_lo[q][i : i + 1], 0.0)
             ).astype(BF16)
-            here = src_t[:, q * LANES : (q + 1) * LANES]
-            right.append(jnp.concatenate([here, pick, pick, near], axis=0))
+            right.append(jnp.concatenate([pick, pick, near], axis=0))
         rights.append(jnp.concatenate(right, axis=1))
-    wave = WAVE
+    hidden = []
+    for members, right in zip(chunks, rights):
+        base = [src_proj[:, q * LANES : (q + 1) * LANES] for _, q in members]
+        hidden.append(dot(a, right) + jnp.concatenate(base, axis=1))
+    hidden = [half_silu(h).astype(BF16) for h in hidden]
+    low = [dot(w2, h) for h in hidden]
+    low = [half_silu(h).astype(BF16) for h in low]
+    lifted = [dot(w3, h) for h in low]
+    gates = [jax.nn.sigmoid(v[width : width + 1] + v[width + 1 : width + 2]) for v in lifted]
     total = jnp.zeros((2 * rows, width), F32)
+    for members, g, m in zip(chunks, gates, low):
+        left = []
+        for n, (i, q) in enumerate(members):
+            cut = slice(n * LANES, (n + 1) * LANES)
+            kept = jnp.where(trow == i, g[:, cut] * keep[q], 0.0)
+            left.append(jnp.concatenate(split2(kept), axis=0))
+        total = total + lax.dot_general(
+            jnp.concatenate(left, axis=1),
+            m,
+            (((1,), (1,)), ((), ())),
+            preferred_element_type=F32,
+        )
     weight_rows = {}
-    for at in range(0, len(chunks), wave):
-        now = range(at, min(at + wave, len(chunks)))
-        hidden = [dot(a, rights[k]) for k in now]
-        hidden = [half_silu(h).astype(BF16) for h in hidden]
-        low = [dot(w2, h) for h in hidden]
-        low = [half_silu(h).astype(BF16) for h in low]
-        lifted = [dot(w3, h) for h in low]
-        gates = [jax.nn.sigmoid(v[width : width + 1] + v[width + 1 : width + 2]) for v in lifted]
-        for k, g, m in zip(now, gates, low):
-            left = []
-            for n, (i, q) in enumerate(chunks[k]):
-                cut = slice(n * LANES, (n + 1) * LANES)
-                kept = jnp.where(trow == i, g[:, cut] * keep[q], 0.0)
-                left.append(jnp.concatenate(split2(kept), axis=0))
-            total = total + lax.dot_general(
-                jnp.concatenate(left, axis=1),
-                m,
-                (((1,), (1,)), ((), ())),
-                preferred_element_type=F32,
-            )
-        for k, v in zip(now, lifted):
-            v = half_silu(v[:width])
+
+    def weigh(picked):
+        for k in picked:
+            v = half_silu(lifted[k][:width])
             for n, (i, q) in enumerate(chunks[k]):
                 cut = slice(n * LANES, (n + 1) * LANES)
                 weight_rows[i, q] = jnp.sum(v[:, cut] * ww, axis=0, keepdims=True)
+
+    third = len(chunks) // SPLIT
     message_mean = ((total[:rows] + total[rows:]) * mean_scale).astype(BF16)
     node_pre = node_part + dot(message_mean, w_node[width:, :])
+    weigh(range(third))
     node_hidden = half_silu(node_pre * 0.5).astype(BF16)
-    feat_out[...] = (x.astype(F32) + dot(node_hidden, w_out[...])).astype(BF16)
+    change = dot(node_hidden, w_out[...])
+    weigh(range(third, len(chunks)))
+    feat_out[...] = (x.astype(F32) + change).astype(BF16)
     sums = [jnp.zeros((rows, 1), F32)] * 3
     for q in range(parts):
         weight = jnp.concatenate([weight_rows[i, q] for i in range(rows)], axis=0) * keep[q]
@@ -184,7 +201,7 @@
     sent, lines, table = pl.pallas_call(
         pack_body,
         out_shape=(
-            pltpu.VMEM((devices, rows + 8, width), BF16),
+            pltpu.VMEM((devices, rows // SLAB + 1, SLAB, width), BF16),
             pltpu.VMEM((8, width), F32),
             pltpu.SMEM(pair_table.shape, pair_table.dtype),
         ),

time: 20 us -> 19.6 us (0.980)
  blocking collectives: 16.1 us -> 15.8 us
    all_to_all x1, blocking collectives: 16.1 us -> 15.8 us  [shards(): far = lax.all_to_all(sent, ('blk', 'edge'), 0, 0, tiled=True)]
where the time goes in v3:
time: 19.6 us; the launch traced here: 19.4 us
  blocking collectives  15.8 us (81%)
  Pallas kernels  2.87 us (15%)
  between operations  0.72 us (4%)
    all_to_all x1, blocking collectives, shards(): far = lax.all_to_all(sent, ('blk', 'edge'), 0, 0, tiled=True)  15.8 us
    pallas_call x1, Pallas kernels, shards(): pl.pallas_call(body, out_shape=(jax.ShapeDtypeStruct((rows, width), BF16)...  1.98 us
    pallas_call x1, Pallas kernels, shards(): pl.pallas_call(pack_body, out_shape=(pltpu.VMEM((devices, rows // SLAB +...  0.89 us

profile of v3, /device:TPU:0, one launch (start us, length us, event | category | flops | bytes accessed | tf_op | source)
XLA Modules:
  0.0 19.4 jit_solution(16778778279162416470)
XLA Ops:
  0.6 0.9 %pack.1 = (bf16[32,5,4,128]{3,2,1,0:T(4,128)(2,1)S(1)}, f32[8,128]{1,0:T(8,128)S(1)}, s32[3,16]{1,0:T(4,128)S(4)}) custom-call(bf16[16,128]{1,0:T(8,128)(2,1)} %feat.1, bf16[3,16]{1,0:T(4,128)(2,1)} %coords.1, s32[3,16]{1,0:T(4,128)} %table.1, f32[1,128]{1,0:T(1,128)} %bitcast.4, f32[1,128]{1,0:T(1,128)} %bitcast.5, f32[1,128]{1,0:T(1,128)} %bitcast.6, ...), custom_call_target="tpu_custom_call" | custom-call | tf_op jit(solution)/shard_map/pack/pallas_call | solution.py:201
  1.5 0.0 copy-start
  1.5 0.0 copy-start.1
  1.6 0.0 copy-start.2
  1.6 0.0 copy-start.3
  1.6 0.0 copy-start.4
  1.6 0.0 copy-start.5
  1.6 15.8 %all_to_all.5.refs_1_ = bf16[32,5,4,128]{3,2,1,0:T(4,128)(2,1)S(1)} all-to-all(bf16[32,5,4,128]{3,2,1,0:T(4,128)(2,1)S(1)} %get-tuple-element.6), channel_id=1, replica_groups=mesh['blk'=16,'edge'=2] {'blk','edge'}, dimensions={0} | all-to-all | bytes 327680 | tf_op jit(solution)/shard_map/all_to_all | solution.py:213
  17.4 0.0 copy-done
  17.4 0.0 copy-done.1
  17.4 0.0 copy-done.2
  17.4 0.0 copy-done.3
  17.4 0.0 copy-done.4
  17.4 0.0 copy-done.5
  17.4 2.0 %edges.1 = (bf16[16,128]{1,0:T(8,128)(2,1)}, f32[3,16]{1,0:T(4,128)}) custom-call(s32[3,16]{1,0:T(4,128)S(4)} %get-tuple-element.5.refs_0_, bf16[32,5,4,128]{3,2,1,0:T(4,128)(2,1)S(1)} %all_to_all.5.refs_1_, f32[8,128]{1,0:T(8,128)S(1)} %get-tuple-element.7.refs_2_, bf16[128,128]{1,0:T(8,128)(2,1)S(1)} %copy-done.1, bf16[128,128]{1,0:T(8,128)(2,1)S(1)} %copy-done.2, ...), custom_call_target="tpu_custom_call" | custom-call | tf_op jit(solution)/shard_map/edges/pallas_call | solution.py:218
Async XLA Ops:
  1.5 15.8 %copy-start = (bf16[256,128]{1,0:T(8,128)(2,1)S(1)}, bf16[256,128]{1,0:T(8,128)(2,1)}, u32[]{:S(2)}) copy-start(bf16[256,128]{1,0:T(8,128)(2,1)} %refs_7_.1) | copy-start | bytes 196612
  1.5 15.8 %copy-start.1 = (bf16[128,128]{1,0:T(8,128)(2,1)S(1)}, bf16[128,128]{1,0:T(8,128)(2,1)}, u32[]{:S(2)}) copy-start(bf16[128,128]{1,0:T(8,128)(2,1)} %refs_3_.1) | copy-start | bytes 98308
  1.6 15.8 %copy-start.2 = (bf16[128,128]{1,0:T(8,128)(2,1)S(1)}, bf16[128,128]{1,0:T(8,128)(2,1)}, u32[]{:S(2)}) copy-start(bf16[128,128]{1,0:T(8,128)(2,1)} %refs_4_.1) | copy-start | bytes 98308
  1.6 15.8 %copy-start.3 = (bf16[128,128]{1,0:T(8,128)(2,1)S(1)}, bf16[128,128]{1,0:T(8,128)(2,1)}, u32[]{:S(2)}) copy-start(bf16[128,128]{1,0:T(8,128)(2,1)} %refs_5_.1) | copy-start | bytes 98308
  1.6 15.8 %copy-start.4 = (bf16[128,128]{1,0:T(8,128)(2,1)S(1)}, bf16[128,128]{1,0:T(8,128)(2,1)}, u32[]{:S(2)}) copy-start(bf16[128,128]{1,0:T(8,128)(2,1)} %refs_6_.1) | copy-start | bytes 98308
  1.6 15.8 %copy-start.5 = (bf16[128,128]{1,0:T(8,128)(2,1)S(1)}, bf16[128,128]{1,0:T(8,128)(2,1)}, u32[]{:S(2)}) copy-start(bf16[128,128]{1,0:T(8,128)(2,1)} %refs_8_.1) | copy-start | bytes 98308

commit v4 on v3

--- a/solution.py
+++ b/solution.py
@@ -27,7 +27,9 @@
     return h + h * jnp.tanh(h)
 
 
-def pack_body(feat, coords, table, w_dist, edge_bias, w_gate, w_weight, sent, lines, table_out):
+def pack_body(feat, coords, table, w_dist, edge_bias, w_gate, w_weight, *rest):
+    weights = rest[: (len(rest) - 3) // 2]
+    sent, lines, table_out = rest[len(weights) : len(weights) + 3]
     rows, width = feat.shape
     spot = jnp.concatenate([coords[...].astype(F32), jnp.zeros((SLAB - 3, rows), F32)], axis=0)
     spot = jnp.concatenate([spot, jnp.zeros((SLAB, width - rows), F32)], axis=1)
@@ -39,11 +41,12 @@
     for r in range(table.shape[0]):
         for b in range(table.shape[1]):
             table_out[r, b] = table[r, b]
+    for near, weight in zip(rest[len(weights) + 3 :], weights):
+        near[...] = weight[...]
 
 
 def edge_body(
     table,
-    far,
     lines,
     w_tgt,
     w_src,
@@ -51,25 +54,25 @@
     w_coord,
     w_node,
     w_out,
-    feat_out,
-    coord_out,
-    *,
+    *rest,
     edge_parts,
     mean_scale,
 ):
+    far = rest[:edge_parts]
+    feat_out, coord_out = rest[edge_parts:]
     rows, width = feat_out.shape
     rounds = table.shape[0]
     block = lax.axis_index("blk")
-    part = lax.axis_index("edge")
+    last = lax.axis_size("blk") - 1
     blocks = [block] + [table[r, block] for r in range(rounds)]
-    places = [h * edge_parts + e for h in blocks for e in range(edge_parts)]
+    places = [(e, last - h) for h in blocks for e in range(edge_parts)]
     slabs = rows // SLAB
 
     def feats(p):
-        return [far[p, k] for k in range(slabs)]
+        return [far[p[0]][p[1], k] for k in range(slabs)]
 
     def spots_of(p):
-        return far[p, slabs].astype(F32)
+        return far[p[0]][p[1], slabs].astype(F32)
 
     parts = rows * len(places) // LANES
     half = jnp.asarray(0.5, BF16)
@@ -77,7 +80,7 @@
     src_t = jnp.concatenate([f for p in places for f in feats(p)], axis=0).T
     spots = jnp.concatenate([spots_of(p)[:, :rows] for p in places], axis=1)
 
-    own = block * edge_parts + part
+    own = places[0]
     x = jnp.concatenate(feats(own), axis=0)
     w_dist, edge_bias, w_gate, w_weight = (lines[k : k + 1, :] for k in range(4))
     tgt_hi, tgt_lo = split2((dot(x, w_tgt[...]) + edge_bias) * 0.5)
@@ -106,7 +109,7 @@
         rad = off[0] * off[0] + off[1] * off[1] + off[2] * off[2]
         scale = 1.0 / (jnp.sqrt(rad) + 1.0)
         unit.append([o * scale for o in off])
-        keep.append(jnp.where(lane + q * LANES == part * rows + trow, 0.0, 1.0))
+        keep.append(jnp.where(lane + q * LANES == trow, 0.0, 1.0))
         hi = rad.astype(BF16).astype(F32)
         r_hi.append(hi)
         r_lo.append(rad - hi)
@@ -189,7 +192,7 @@
 ):
     rows, width = node_feat.shape
     edge_parts = lax.axis_size("edge")
-    devices = lax.axis_size("blk") * edge_parts
+    blocks = lax.axis_size("blk")
     rounds = pair_table.shape[0]
     mean_scale = 1.0 / ((rounds + 1) * rows * edge_parts - 1)
     vmem = pl.BlockSpec(memory_space=pltpu.VMEM)
@@ -198,19 +201,25 @@
     line = lambda v: v.reshape(1, -1)
     small = (line(w_dist), line(edge_bias), line(w_gate), line(w_weight))
     hold = lambda v: pltpu.with_memory_space_constraint(v, pltpu.HBM)
-    sent, lines, table = pl.pallas_call(
+    weights = (w_tgt, w_src, w_edge, w_coord, w_node_in, w_node_out)
+    sent, lines, table, *near = pl.pallas_call(
         pack_body,
         out_shape=(
-            pltpu.VMEM((devices, rows // SLAB + 1, SLAB, width), BF16),
+            pltpu.VMEM((blocks, rows // SLAB + 1, SLAB, width), BF16),
             pltpu.VMEM((8, width), F32),
             pltpu.SMEM(pair_table.shape, pair_table.dtype),
-        ),
-        in_specs=[vmem] * 2 + [smem] + [vmem] * 4,
-        out_specs=(vmem, vmem, smem),
+        )
+        + tuple(pltpu.VMEM(w.shape, w.dtype) for w in weights),
+        in_specs=[vmem] * 2 + [smem] + [vmem] * (4 + len(weights)),
+        out_specs=(vmem, vmem, smem) + (vmem,) * len(weights),
         compiler_params=params,
         name="pack",
-    )(*(hold(v) for v in (node_feat, coords, pair_table) + small))
-    far = lax.all_to_all(sent, ("blk", "edge"), 0, 0, tiled=True)
+    )(*(hold(v) for v in (node_feat, coords, pair_table) + small + weights))
+    order = [list(range(blocks))[::-1]]
+    far = [lax.all_to_all(sent, "blk", 0, 0, tiled=True, axis_index_groups=order)]
+    for step in range(1, edge_parts):
+        ring = [(e, (e + step) % edge_parts) for e in range(edge_parts)]
+        far.append(lax.ppermute(far[0], "edge", ring))
 
     def body(*refs):
         edge_body(*refs, edge_parts=edge_parts, mean_scale=mean_scale)
@@ -221,20 +230,15 @@
             jax.ShapeDtypeStruct((rows, width), BF16),
             jax.ShapeDtypeStruct((3, rows), F32),
         ),
-        in_specs=[smem] + [vmem] * 8,
+        in_specs=[smem] + [vmem] * (7 + edge_parts),
         out_specs=(vmem, vmem),
         compiler_params=params,
         name="edges",
     )(
         table,
-        far,
         lines,
-        w_tgt,
-        w_src,
-        w_edge,
-        w_coord,
-        w_node_in,
-        w_node_out,
+        *near,
+        *far,
     )
 
 

time: 19.6 us -> 17.7 us (0.903)
  blocking collectives: 15.8 us -> 12.5 us
  waiting for transfers between devices: 0 us -> 1.27 us
    all_to_all x1, blocking collectives: 15.8 us -> 12.5 us  [shards(): lax.all_to_all(sent, 'blk', 0, 0, tiled=True, axis_index_groups=order)]
    ppermute x0 -> x1, waiting for transfers between devices: none -> 1.27 us  [shards(): far.append(lax.ppermute(far[0], 'edge', ring))]
  transfers between devices with their start and end apart: 0 -> 1, of which waited for: 0 -> 1; matrix products, arithmetic and copies ran while one was open for 0% -> 0% of each run, Pallas kernels for 0% -> 0%
where the time goes in v4:
time: 17.7 us; the launch traced here: 17.5 us
  blocking collectives  12.5 us (71%)
  Pallas kernels  3.06 us (17%)
  waiting for transfers between devices  1.27 us (7%)
  between operations  0.64 us (4%)
    all_to_all x1, blocking collectives, shards(): lax.all_to_all(sent, 'blk', 0, 0, tiled=True, axis_index_groups=order)  12.5 us
    pallas_call x1, Pallas kernels, shards(): pl.pallas_call(body, out_shape=(jax.ShapeDtypeStruct((rows, width), BF16)...  1.98 us
    ppermute x1, waiting for transfers between devices, shards(): far.append(lax.ppermute(far[0], 'edge', ring))  1.27 us
    pallas_call x1, Pallas kernels, shards(): pl.pallas_call(pack_body, out_shape=(pltpu.VMEM((blocks, rows // SLAB + 1...  1.08 us
  transfers between devices with their start and end apart: 1, of which 1 were waited for; matrix products, arithmetic and copies ran while one was open for 0% of the time, Pallas kernels for 0%

profile of v4, /device:TPU:0, one launch (start us, length us, event | category | flops | bytes accessed | tf_op | source)
XLA Modules:
  0.0 17.5 jit_solution(11897231061444523879)
XLA Ops:
  0.6 1.1 %pack.1 = (bf16[16,5,4,128]{3,2,1,0:T(4,128)(2,1)S(1)}, f32[8,128]{1,0:T(8,128)S(1)}, s32[3,16]{1,0:T(4,128)S(4)}, bf16[128,128]{1,0:T(8,128)(2,1)S(1)}, bf16[12...) custom-call(bf16[16,128]{1,0:T(8,128)(2,1)} %feat.1, ...), custom_call_target="tpu_custom_call" | custom-call | tf_op jit(solution)/shard_map/pack/pallas_call | solution.py:205
  1.7 12.5 %all_to_all.5.refs_8_ = bf16[16,5,4,128]{3,2,1,0:T(4,128)(2,1)S(1)} all-to-all(bf16[16,5,4,128]{3,2,1,0:T(4,128)(2,1)S(1)} %get-tuple-element.19), channel_id=1, replica_groups={{30,28,26,24,22,20,18,16,14,12,10,8,6,4,2,0},{31,29,27,25,23,21,19,17,1..., dimensions={0} | all-to-all | bytes 163840 | tf_op jit(solution)/shard_map/all_to_all | solution.py:219
  14.2 0.0 collective-permute-start
  14.3 1.3 %collective-permute-done.refs_9_ = bf16[16,5,4,128]{3,2,1,0:T(4,128)(2,1)S(1)} collective-permute-done((bf16[16,5,4,128]{3,2,1,0:T(4,128)(2,1)S(1)}, bf16[16,5,4,128]{3,2,1,0:T(4,128)(2,1)S(1)}, u32[]{:S(2)}, u32[]{:S(2)}) %collective-permute-start) | collective-permute-done | bytes 81952 | tf_op jit(solution)/shard_map/ppermute | solution.py:222
  15.5 2.0 %edges.1 = (bf16[16,128]{1,0:T(8,128)(2,1)}, f32[3,16]{1,0:T(4,128)}) custom-call(s32[3,16]{1,0:T(4,128)S(4)} %get-tuple-element.11.refs_0_, f32[8,128]{1,0:T(8,128)S(1)} %get-tuple-element.12.refs_1_, bf16[128,128]{1,0:T(8,128)(2,1)S(1)} %get-tuple-element.13.refs_2_, bf16[128,128]{1,0:T(8,128)(2,1)S(1)} %get-tuple-element.14.refs_3_, ...), custom_call_target="tpu_custom_call" | custom-call | tf_op jit(solution)/shard_map/edges/pallas_call | solution.py:227
Async XLA Ops:
  14.2 1.3 %collective-permute-start = (bf16[16,5,4,128]{3,2,1,0:T(4,128)(2,1)S(1)}, bf16[16,5,4,128]{3,2,1,0:T(4,128)(2,1)S(1)}, u32[]{:S(2)}, u32[]{:S(2)}) collective-permute-start(bf16[16,5,4,128]{3,2,1,0:T(4,128)(2,1)S(1)} %all_to_all.5.refs_8_), channel_id=1, source_target_pairs={{0,1},{1,0},{2,3},{3,2},{4,5},{5,4},{6,7},{7,6},{8,9},{9,8},{10,11... | collective-permute-start | bytes 245768 | tf_op jit(solution)/shard_map/ppermute | solution.py:222

commit v5 on v4

v5 whole, which is shorter than its diff:
```python
import jax
import jax.numpy as jnp
from jax import lax
from jax.experimental import pallas as pl
from jax.experimental.pallas import tpu as pltpu
from jax.sharding import PartitionSpec as P

F32 = jnp.float32
BF16 = jnp.bfloat16
LANES = 128
VMEM_BYTES = 24 * 2**20
SLAB = 4


def split2(x):
    hi = x.astype(BF16)
    lo = (x - hi.astype(F32)).astype(BF16)
    return hi, lo


def dot(a, b):
    return jnp.dot(a, b, preferred_element_type=F32)


def half_silu(h):
    return h + h * jnp.tanh(h)


def pack_body(feat, coords, table, w_dist, edge_bias, w_gate, w_weight, *rest):
    weights = rest[: (len(rest) - 3) // 2]
    sent, lines, table_out = rest[len(weights) : len(weights) + 3]
    rows, width = feat.shape
    spot = jnp.concatenate([coords[...].astype(F32), jnp.zeros((SLAB - 3, rows), F32)], axis=0)
    spot = jnp.concatenate([spot, jnp.zeros((SLAB, width - rows), F32)], axis=1)
    slabs = [feat[k : k + SLAB, :] for k in range(0, rows, SLAB)] + [spot.astype(BF16)]
    for k, slab in enumerate(slabs):
        sent[:, k] = jnp.broadcast_to(slab[None], (sent.shape[0],) + slab.shape)
    for k, line in enumerate((w_dist, edge_bias, w_gate, w_weight)):
        lines[k : k + 1, :] = line[...]
    for r in range(table.shape[0]):
        for b in range(table.shape[1]):
            table_out[r, b] = table[r, b]
    for near, weight in zip(rest[len(weights) + 3 :], weights):
        near[...] = weight[...]


def half_edges(far, slots, rows, place, keep, mats):
    a, w_src_t, w2, w3, ww = mats
    width = w2.shape[0]
    slabs = rows // SLAB
    sources = rows * len(slots)
    fold = LANES // sources
    groups = rows // fold
    src = [far[p, k] for p in slots for k in range(slabs)]
    src_proj = dot(w_src_t, jnp.concatenate(src * fold, axis=0).T)
    spots = [far[p, slabs].astype(F32)[:, :rows] for p in slots]
    spots = jnp.concatenate(spots * fold, axis=1)
    off = [place[c] - spots[c : c + 1] for c in range(3)]
    rad = off[0] * off[0] + off[1] * off[1] + off[2] * off[2]
    scale = 1.0 / (jnp.sqrt(rad) + 1.0)
    unit = [o * scale for o in off]
    r_hi = rad.astype(BF16).astype(F32)
    r_lo = rad - r_hi
    lrow = lax.broadcasted_iota(jnp.int32, (16, LANES), 0)
    trow = lax.broadcasted_iota(jnp.int32, (rows, LANES), 0)
    upper = groups * (lax.broadcasted_iota(jnp.int32, (rows, LANES), 1) // sources)
    picks = [trow == g + upper for g in range(groups)]
    chunks = [list(range(at, min(at + 2, groups))) for at in range(0, groups, 2)]
    hidden = []
    for members in chunks:
        right = []
        for g in members:
            pick = jnp.where(picks[g], 1.0, 0.0).astype(BF16)
            near = jnp.where(
                lrow < 2, r_hi[g : g + 1], jnp.where(lrow == 2, r_lo[g : g + 1], 0.0)
            ).astype(BF16)
            right.append(jnp.concatenate([pick, pick, near], axis=0))
        base = jnp.concatenate([src_proj] * len(members), axis=1)
        hidden.append(dot(a, jnp.concatenate(right, axis=1)) + base)
    hidden = [half_silu(h).astype(BF16) for h in hidden]
    low = [dot(w2, h) for h in hidden]
    low = [half_silu(h).astype(BF16) for h in low]
    lifted = [dot(w3, h) for h in low]
    gates = [jax.nn.sigmoid(v[width : width + 1] + v[width + 1 : width + 2]) for v in lifted]
    total = jnp.zeros((2 * rows, width), F32)
    for members, gate, m in zip(chunks, gates, low):
        left = []
        for n, g in enumerate(members):
            one = gate[:, n * LANES : (n + 1) * LANES]
            if keep is not None:
                one = one * keep[g : g + 1]
            left.append(jnp.concatenate(split2(jnp.where(picks[g], one, 0.0)), axis=0))
        total = total + lax.dot_general(
            jnp.concatenate(left, axis=1),
            m,
            (((1,), (1,)), ((), ())),
            preferred_element_type=F32,
        )

    def directions():
        weight = []
        for members, v in zip(chunks, lifted):
            v = half_silu(v[:width])
            for n in range(len(members)):
                cut = slice(n * LANES, (n + 1) * LANES)
                weight.append(jnp.sum(v[:, cut] * ww, axis=0, keepdims=True))
        weight = jnp.concatenate(weight, axis=0)
        if keep is not None:
            weight = weight * keep
        return [u * weight for u in unit]

    return total, directions


def near_body(
    table,
    lines,
    w_tgt,
    w_src,
    w_edge,
    w_coord,
    w_node,
    far,
    a_out,
    src_out,
    w2_out,
    w3_out,
    ww_out,
    place_out,
    node_out,
    total_out,
    way_out,
):
    groups = place_out.shape[1]
    rows, width = node_out.shape
    slabs = rows // SLAB
    slots = slots_of(table)
    fold = rows // groups
    sources = LANES // fold
    half = jnp.asarray(0.5, BF16)
    x = jnp.concatenate([far[slots[0], k] for k in range(slabs)], axis=0)
    w_dist, edge_bias, w_gate, w_weight = (lines[k : k + 1, :] for k in range(4))
    tgt_hi, tgt_lo = split2((dot(x, w_tgt[...]) + edge_bias) * 0.5)
    dist = w_dist * 0.5
    d_hi = dist.astype(BF16).astype(F32)
    urow = lax.broadcasted_iota(jnp.int32, (16, width), 0)
    tail = jnp.where(urow == 1, dist - d_hi, jnp.where(urow < 3, d_hi, 0.0)).astype(BF16)
    a = jnp.concatenate([tgt_hi, tgt_lo, tail], axis=0).T
    w_src_t = (w_src[...] * half).T
    w2 = (w_edge[...] * half).T
    g_hi = w_gate.astype(BF16).astype(F32)
    g_rows = jnp.where(urow == 0, g_hi, jnp.where(urow == 1, w_gate - g_hi, 0.0)).astype(BF16)
    w3 = jnp.concatenate([(w_coord[...] * half).T, g_rows], axis=0)
    ww = jnp.broadcast_to(w_weight, (LANES, width)).T
    spot = far[slots[0], slabs].astype(F32)
    col = jnp.concatenate([spot, jnp.zeros((8 - SLAB, width), F32)], axis=0).T
    lane = lax.broadcasted_iota(jnp.int32, (groups, LANES), 1)
    grow = lax.broadcasted_iota(jnp.int32, (groups, LANES), 0)
    place = []
    for c in range(3):
        spread = jnp.broadcast_to(col[:groups, c : c + 1], (groups, LANES))
        for f in range(1, fold):
            there = col[f * groups : (f + 1) * groups, c : c + 1]
            spread = jnp.where(lane >= f * sources, there, spread)
        place.append(spread)
    keep = jnp.where(lane % sources == grow + groups * (lane // sources), 0.0, 1.0)
    a_out[...] = a
    src_out[...] = w_src_t
    w2_out[...] = w2
    w3_out[...] = w3
    ww_out[...] = ww
    node_out[...] = dot(x, w_node[:width, :])
    total, directions = half_edges(
        far, slots, rows, place, keep, (a, w_src_t, w2, w3, ww)
    )
    total_out[...] = total
    for c, way in enumerate(directions()):
        place_out[c] = place[c]
        way_out[c] = way


def slots_of(table):
    block = lax.axis_index("blk")
    last = lax.axis_size("blk") - 1
    return [last - block] + [last - table[r, block] for r in range(table.shape[0])]


def far_body(
    table,
    a_ref,
    src_ref,
    w2_ref,
    w3_ref,
    ww_ref,
    place_ref,
    node_ref,
    total_ref,
    way_ref,
    w_node,
    w_out,
    own,
    *rest,
    mean_scale,
):
    others = rest[:-2]
    feat_out, coord_out = rest[-2:]
    rows, width = feat_out.shape
    groups = place_ref.shape[1]
    fold = rows // groups
    sources = LANES // fold
    slabs = rows // SLAB
    slots = slots_of(table)
    mats = (a_ref[...], src_ref[...], w2_ref[...], w3_ref[...], ww_ref[...])
    place = [place_ref[c] for c in range(3)]
    total = total_ref[...]
    way = [way_ref[c] for c in range(3)]
    pending = []
    for far in others:
        more, directions = half_edges(far, slots, rows, place, None, mats)
        total = total + more
        pending.append(directions)
    message_mean = ((total[:rows] + total[rows:]) * mean_scale).astype(BF16)
    node_pre = node_ref[...] + dot(message_mean, w_node[width:, :])
    node_hidden = half_silu(node_pre * 0.5).astype(BF16)
    change = dot(node_hidden, w_out[...])
    for directions in pending:
        way = [w + more for w, more in zip(way, directions())]
    x = jnp.concatenate([own[slots[0], k] for k in range(slabs)], axis=0)
    feat_out[...] = (x.astype(F32) + change).astype(BF16)
    lane = lax.broadcasted_iota(jnp.int32, (groups, LANES), 1)
    sums = []
    for w in way:
        parts = [
            jnp.sum(jnp.where(lane // sources == f, w, 0.0), axis=1, keepdims=True)
            for f in range(fold)
        ]
        sums.append(jnp.concatenate(parts, axis=0))
    wide = lax.broadcasted_iota(jnp.int32, (rows, LANES), 1)
    side = jnp.where(wide == 0, sums[0], jnp.where(wide == 1, sums[1], sums[2]))
    spot = own[slots[0], slabs].astype(F32)
    coord_out[...] = spot[:3, :rows] + side.T[:3] * mean_scale


def shards(
    node_feat,
    coords,
    pair_table,
    w_tgt,
    w_src,
    w_dist,
    edge_bias,
    w_edge,
    w_gate,
    w_coord,
    w_weight,
    w_node_in,
    w_node_out,
):
    rows, width = node_feat.shape
    edge_parts = lax.axis_size("edge")
    blocks = lax.axis_size("blk")
    rounds = pair_table.shape[0]
    mean_scale = 1.0 / ((rounds + 1) * rows * edge_parts - 1)
    vmem = pl.BlockSpec(memory_space=pltpu.VMEM)
    smem = pl.BlockSpec(memory_space=pltpu.SMEM)
    params = pltpu.CompilerParams(vmem_limit_bytes=VMEM_BYTES)
    line = lambda v: v.reshape(1, -1)
    small = (line(w_dist), line(edge_bias), line(w_gate), line(w_weight))
    hold = lambda v: pltpu.with_memory_space_constraint(v, pltpu.HBM)
    weights = (w_tgt, w_src, w_edge, w_coord, w_node_in, w_node_out)
    sent, lines, table, *near = pl.pallas_call(
        pack_body,
        out_shape=(
            pltpu.VMEM((blocks, rows // SLAB + 1, SLAB, width), BF16),
            pltpu.VMEM((8, width), F32),
            pltpu.SMEM(pair_table.shape, pair_table.dtype),
        )
        + tuple(pltpu.VMEM(w.shape, w.dtype) for w in weights),
        in_specs=[vmem] * 2 + [smem] + [vmem] * (4 + len(weights)),
        out_specs=(vmem, vmem, smem) + (vmem,) * len(weights),
        compiler_params=params,
        name="pack",
    )(*(hold(v) for v in (node_feat, coords, pair_table) + small + weights))
    order = [list(range(blocks))[::-1]]
    far = [lax.all_to_all(sent, "blk", 0, 0, tiled=True, axis_index_groups=order)]
    for step in range(1, edge_parts):
        ring = [(e, (e + step) % edge_parts) for e in range(edge_parts)]
        far.append(lax.ppermute(far[0], "edge", ring))

    w_tgt, w_src, w_edge, w_coord, w_node, w_out = near
    fold = LANES // (rows * (rounds + 1))
    groups = rows // fold
    prepared = pl.pallas_call(
        near_body,
        out_shape=(
            pltpu.VMEM((width, 2 * rows + 16), BF16),
            pltpu.VMEM((width, width), BF16),
            pltpu.VMEM((width, width), BF16),
            pltpu.VMEM((width + 16, width), BF16),
            pltpu.VMEM((width, LANES), F32),
            pltpu.VMEM((3, groups, LANES), F32),
            pltpu.VMEM((rows, width), F32),
            pltpu.VMEM((2 * rows, width), F32),
            pltpu.VMEM((3, groups, LANES), F32),
        ),
        in_specs=[smem] + [vmem] * 7,
        out_specs=(vmem,) * 9,
        compiler_params=params,
        cost_estimate=pl.CostEstimate(
            flops=4 * rows * rows * (rounds + 1) * width * width,
            transcendentals=3 * rows * rows * (rounds + 1) * width,
            bytes_accessed=0,
        ),
        name="near",
    )(table, lines, w_tgt, w_src, w_edge, w_coord, w_node, far[0])

    def body(*refs):
        far_body(*refs, mean_scale=mean_scale)

    return pl.pallas_call(
        body,
        out_shape=(
            jax.ShapeDtypeStruct((rows, width), BF16),
            jax.ShapeDtypeStruct((3, rows), F32),
        ),
        in_specs=[smem] + [vmem] * (11 + edge_parts),
        out_specs=(vmem, vmem),
        compiler_params=params,
        name="far",
    )(table, *prepared, w_node, w_out, *far)


def solution(mesh):
    whole = P()
    placed = (P(("blk", "edge"), None), P(None, ("blk", "edge"))) + (whole,) * 11
    return jax.shard_map(
        shards,
        mesh=mesh,
        in_specs=placed,
        out_specs=(P(("blk", "edge"), None), P(None, ("blk", "edge"))),
        check_vma=False,
    )
```

time: 17.7 us -> 17.4 us (0.983)
  waiting for transfers between devices: 1.27 us -> 0.33 us
  Pallas kernels: 3.06 us -> 3.68 us
    ppermute x1, waiting for transfers between devices: 1.27 us -> 0.33 us  [shards(): far.append(lax.ppermute(far[0], 'edge', ring))]
    pallas_call x0 -> x1, Pallas kernels: none -> 0.94 us  [shards(): pl.pallas_call(near_body, out_shape=(pltpu.VMEM((width, 2 * rows + 16), B...]
    pallas_call x1, Pallas kernels: 1.98 us -> 1.66 us  [shards(): pl.pallas_call(body, out_shape=(jax.ShapeDtypeStruct((rows, width), BF16)...]
  transfers between devices with their start and end apart: 1 -> 1, of which waited for: 1 -> 1; matrix products, arithmetic and copies ran while one was open for 0% -> 0% of each run, Pallas kernels for 0% -> 5%
where the time goes in v5:
time: 17.4 us; the launch traced here: 17.2 us
  blocking collectives  12.5 us (72%)
  Pallas kernels  3.68 us (21%)
  between operations  0.65 us (4%)
  waiting for transfers between devices  0.33 us (2%)
    all_to_all x1, blocking collectives, shards(): lax.all_to_all(sent, 'blk', 0, 0, tiled=True, axis_index_groups=order)  12.5 us
    pallas_call x1, Pallas kernels, shards(): pl.pallas_call(body, out_shape=(jax.ShapeDtypeStruct((rows, width), BF16)...  1.66 us
    pallas_call x1, Pallas kernels, shards(): pl.pallas_call(pack_body, out_shape=(pltpu.VMEM((blocks, rows // SLAB + 1...  1.08 us
    pallas_call x1, Pallas kernels, shards(): pl.pallas_call(near_body, out_shape=(pltpu.VMEM((width, 2 * rows + 16), B...  0.94 us
  transfers between devices with their start and end apart: 1, of which 1 were waited for; matrix products, arithmetic and copies ran while one was open for 0% of the time, Pallas kernels for 5%

profile of v5, /device:TPU:0, one launch (start us, length us, event | category | flops | bytes accessed | tf_op | source)
XLA Modules:
  0.0 17.2 jit_solution(6521453500844364642)
XLA Ops:
  0.6 1.1 %pack.1 = (bf16[16,5,4,128]{3,2,1,0:T(4,128)(2,1)S(1)}, f32[8,128]{1,0:T(8,128)S(1)}, s32[3,16]{1,0:T(4,128)S(4)}, bf16[128,128]{1,0:T(8,128)(2,1)S(1)}, bf16[12...) custom-call(bf16[16,128]{1,0:T(8,128)(2,1)} %feat.1, ...), custom_call_target="tpu_custom_call" | custom-call | tf_op jit(solution)/shard_map/pack/pallas_call | solution.py:271
  1.7 12.5 %all_to_all.5.far.refs_12_ = bf16[16,5,4,128]{3,2,1,0:T(4,128)(2,1)S(1)} all-to-all(bf16[16,5,4,128]{3,2,1,0:T(4,128)(2,1)S(1)} %get-tuple-element.27), channel_id=1, replica_groups={{30,28,26,24,22,20,18,16,14,12,10,8,6,4,2,0},{31,29,27,25,23,21,19,17,1..., dimensions={0} | all-to-all | bytes 163840 | tf_op jit(solution)/shard_map/all_to_all | solution.py:285
  14.2 0.0 collective-permute-start
  14.3 0.9 %near.1 = (bf16[128,48]{1,0:T(8,128)(2,1)S(1)}, bf16[128,128]{1,0:T(8,128)(2,1)S(1)}, bf16[128,128]{1,0:T(8,128)(2,1)S(1)}, bf16[144,128]{1,0:T(8,128)(2,1)S(1)}...) custom-call(s32[3,16]{1,0:T(4,128)S(4)} %get-tuple-element.20.table., ...), custom_call_target="tpu_custom_call" | custom-call | flops 67108864 | tf_op jit(solution)/shard_map/near/pallas_call | solution.py:293
  15.2 0.3 %collective-permute-done.refs_13_ = bf16[16,5,4,128]{3,2,1,0:T(4,128)(2,1)S(1)} collective-permute-done((bf16[16,5,4,128]{3,2,1,0:T(4,128)(2,1)S(1)}, bf16[16,5,4,128]{3,2,1,0:T(4,128)(2,1)S(1)}, u32[]{:S(2)}, u32[]{:S(2)}) %collective-permute-start) | collective-permute-done | bytes 81952 | tf_op jit(solution)/shard_map/ppermute | solution.py:288
  15.5 1.7 %far.1 = (bf16[16,128]{1,0:T(8,128)(2,1)}, f32[3,16]{1,0:T(4,128)}) custom-call(s32[3,16]{1,0:T(4,128)S(4)} %get-tuple-element.20.table.refs_0_, bf16[128,48]{1,0:T(8,128)(2,1)S(1)} %get-tuple-element.28.refs_1_, bf16[128,128]{1,0:T(8,128)(2,1)S(1)} %get-tuple-element.29.refs_2_, bf16[128,128]{1,0:T(8,128)(2,1)S(1)} %get-tuple-element.30.refs_3_, ...), custom_call_target="tpu_custom_call" | custom-call | tf_op jit(solution)/shard_map/far/pallas_call | solution.py:320
Async XLA Ops:
  14.2 1.3 %collective-permute-start = (bf16[16,5,4,128]{3,2,1,0:T(4,128)(2,1)S(1)}, bf16[16,5,4,128]{3,2,1,0:T(4,128)(2,1)S(1)}, u32[]{:S(2)}, u32[]{:S(2)}) collective-permute-start(bf16[16,5,4,128]{3,2,1,0:T(4,128)(2,1)S(1)} %all_to_all.5.far.refs_12_), channel_id=1, source_target_pairs={{0,1},{1,0},{2,3},{3,2},{4,5},{5,4},{6,7},{7,6},{8,9},{9,8},{10,11... | collective-permute-start | bytes 245768 | tf_op jit(solution)/shard_map/ppermute | solution.py:288
